TPU v7x, 256 devices: a whole 4x4x8 slice. The times are simulated.
256 devices in a mesh: row: 32 (over y, z), col: 8 (over x, core).
Axes of the slice: x: 4, y: 4, z: 8, core: 2. Of those that a mesh axis runs over, the one named last changes fastest.
Arguments:
- sim_window: bfloat16 [6144, 6144], P('row', 'col'), as said below
- sim_rest: bfloat16 [6144, 113856], P('row', 'col'), may hold values from -6 to 6
- joined_partner_pairs: int32 [768, 2], replicated, may hold values from 0 to 6143, as said below
- cluster_member_count: int32 [6144], replicated, may hold values from 1 to 64
Outputs:
- window_out: bfloat16 [6144, 6144], P('row', 'col')
- rest_out: bfloat16 [6144, 113856], P('row', 'col')
Inputs may be any that keep to these rules, and one draw needn't show every extreme that they name: `joined_partner_pairs`: each row is (survivor, partner); no window item appears twice in the whole list. Each aligned block of 192 items holds exactly 24 partners. For any two aligned blocks (possibly the same), at most 3 pairs have their partner in the first and their survivor in the second, and some two blocks have exactly 3. Nearly symmetric: sim_window[i, j] is close to sim_window[j, i].
All inputs are finite; a program needn't handle non-finite values.
Results may differ from a plain program's by a relative error of at most 0.001.
Values may be sent and summed in bfloat16 or wider, within the bound.
No kernel may reach another device: no remote copies, remote signals or barrier semaphores. Data moves between devices by JAX's collectives and lax.ppermute only.
A program may use at most 128 MiB of HBM per device.

v0:
```python
import functools

import jax
import jax.numpy as jnp
from jax import lax
from jax.experimental import pallas as pl
from jax.experimental.pallas import tpu as pltpu
from jax.sharding import PartitionSpec as P


NY, NZ = 4, 8
SEND = 24
CAP = 3
TO_Z = CAP * NY
SLOTS = NY * NZ * CAP
HALVES = 2
BLOCK = 1280
TILE = 256
Z_ORDER, Y_ORDER = (1, 7, 2, 6, 3, 5, 4), (1, 3, 2)
EDGE = 512
SPLIT = 7680
BF = jnp.bfloat16
F32 = jnp.float32
VMEM = pl.BlockSpec(memory_space=pltpu.VMEM)
ANY = pl.BlockSpec(memory_space=pl.ANY)
HBM = pl.BlockSpec(memory_space=pltpu.HBM)


def row_perm(dy, dz):
    return [
        (y * NZ + z, (y + dy) % NY * NZ + (z + dz) % NZ) for y in range(NY) for z in range(NZ)
    ]


def hot(ids, count, on=None):
    mask = ids[None, :] == jnp.arange(count, dtype=jnp.int32)[:, None]
    if on is not None:
        mask = mask & on[None, :]
    return mask.astype(BF)


def join(left, right):
    return lax.dot_general(left, right, (((1,), (1,)), ((), ())), preferred_element_type=F32).astype(BF)


def joins_kernel(kinds, *refs):
    n = len(refs) // 3
    for (row_halves, col_halves), left, right, out in zip(kinds, refs[:n], refs[n : 2 * n], refs[2 * n :]):
        pairs = left.shape[1]
        rows = lax.broadcasted_iota(jnp.int32, (out.shape[0], pairs), 0) // row_halves
        cols = lax.broadcasted_iota(jnp.int32, (out.shape[1], pairs), 0) // col_halves
        at_row = jnp.where(rows == left[...], 1.0, 0.0).astype(BF)
        at_col = jnp.where(cols == right[...], 1.0, 0.0).astype(BF)
        table = lax.dot_general(at_row, at_col, (((1,), (1,)), ((), ())), preferred_element_type=F32)
        if row_halves > 1 and col_halves > 1:
            row = lax.broadcasted_iota(jnp.int32, table.shape, 0) % HALVES
            col = lax.broadcasted_iota(jnp.int32, table.shape, 1) % HALVES
            table = jnp.where(row == col, table, 0.0)
        out[...] = table.astype(BF)


def joins(*tables):
    pairs = tables[0][1].shape[0]
    shapes = [(rows * rh, cols * ch) for (rows, rh), _, (cols, ch), _ in tables]
    return pl.pallas_call(
        functools.partial(joins_kernel, [(t[0][1], t[2][1]) for t in tables]),
        in_specs=[VMEM] * (2 * len(tables)),
        out_specs=[VMEM] * len(tables),
        out_shape=[jax.ShapeDtypeStruct(s, BF) for s in shapes],
        compiler_params=params(8),
        cost_estimate=pl.CostEstimate(
            flops=sum(2 * r * c * pairs for r, c in shapes), bytes_accessed=0, transcendentals=0
        ),
    )(*[t[1][None, :] for t in tables], *[t[3][None, :] for t in tables])


def rank(code):
    order = jnp.arange(code.shape[0], dtype=jnp.int32)
    same = (code[None, :] == code[:, None]) & (order[None, :] < order[:, None])
    return jnp.sum(same.astype(jnp.int32), axis=1)


def item_weights(labels, lasting, vanishing, retained_pair, selected_pair):
    is_last = labels[:, None] == lasting[None, :]
    is_gone = labels[:, None] == vanishing[None, :]
    matched = jnp.sum((is_last | is_gone).astype(F32), axis=1)
    keep = 1.0 - matched + jnp.sum(jnp.where(is_last, retained_pair[None, :], 0.0), axis=1)
    take = jnp.sum(jnp.where(is_last, selected_pair[None, :], 0.0), axis=1)
    return keep, take


def sizes_of(items, counts2d):
    rows = hot(items // 128, counts2d.shape[0])
    lines = lax.dot_general(rows, counts2d, (((0,), (0,)), ((), ())), preferred_element_type=F32)
    lane = (items % 128)[:, None] == jnp.arange(128, dtype=jnp.int32)[None, :]
    return jnp.sum(jnp.where(lane, lines, 0.0), axis=1)


def params(limit_mib):
    return pltpu.CompilerParams(vmem_limit_bytes=limit_mib * 1024 * 1024)


def tiles(start, width, body):
    count = width // TILE

    @pl.loop(0, count, unroll=next((n for n in (5, 4, 3) if count % n == 0), 1))
    def _(t):
        body(pl.ds(pl.multiple_of(start + t * TILE, TILE), TILE))


def only_half(table, q, axis):
    return jnp.where(lax.broadcasted_iota(jnp.int32, table.shape, axis) % HALVES == q, table, jnp.zeros_like(table))


def edge_pieces(rest, start):
    tail = rest.shape[1] - start
    whole = tail // 128 * 128
    return [(at, width) for at, width in ((0, whole), (whole, tail - whole)) if width]


def pick_halves(sel, x, half, outs):
    first, second = (only_half(sel[...], q, 0) for q in range(HALVES))

    def put(cols):
        later = pl.ds(pl.multiple_of(half + cols.start, TILE), TILE)
        out = jnp.dot(first, x[:, cols], preferred_element_type=F32)
        out += jnp.dot(second, x[:, later], preferred_element_type=F32)
        store_rows(outs, cols, out.astype(BF))

    tiles(0, half, put)


def select_a_kernel(start, main, *refs):
    sel, rest, win = refs[:3]
    outs = refs[3:-3]
    held, tail, sems = refs[-3:]
    side = main + EDGE
    copies = []
    for i, at in enumerate(range(0, main, BLOCK)):
        n = min(BLOCK, main - at)
        copies.append(
            pltpu.make_async_copy(rest.at[:, start + at : start + at + n], held.at[:, at : at + n], sems.at[i])
        )
    copies.append(pltpu.make_async_copy(win, held.at[:, side : side + win.shape[1]], sems.at[len(copies)]))
    copies.append(pltpu.make_async_copy(rest.at[:, start + main :], tail, sems.at[len(copies)]))
    for copy in copies:
        copy.start()
    held[:, main : main + EDGE] = jnp.zeros((held.shape[0], EDGE), BF)
    for copy in copies:
        copy.wait()
    held[:, main : main + tail.shape[1]] = tail[...]
    pick_halves(sel, held, held.shape[1] // HALVES, outs)


def select_a(sel, counts, rest, window, start, main):
    rows = rest.shape[0]
    width = main + EDGE + window.shape[1]
    return pl.pallas_call(
        functools.partial(select_a_kernel, start, main),
        in_specs=[VMEM, HBM, HBM],
        out_specs=[VMEM] * len(counts),
        out_shape=[jax.ShapeDtypeStruct((n, width // HALVES), BF) for n in counts],
        scratch_shapes=[
            pltpu.VMEM((rows, width), BF),
            pltpu.VMEM((rows, rest.shape[1] - start - main), BF),
            pltpu.SemaphoreType.DMA((main // BLOCK + 3,)),
        ],
        compiler_params=params(50),
        cost_estimate=pl.CostEstimate(
            flops=2 * sel.shape[0] * rows * width, bytes_accessed=2 * rows * width, transcendentals=0
        ),
        name="select_a",
    )(sel, rest, window)


def select_b_kernel(sel, rest, out):
    pick_halves(sel, rest, out.shape[1], (out,))


def select_b(sel, rest, width):
    return pl.pallas_call(
        select_b_kernel,
        in_specs=[VMEM] * 2,
        out_specs=VMEM,
        out_shape=jax.ShapeDtypeStruct((sel.shape[0], width // HALVES), BF),
        compiler_params=params(8),
        cost_estimate=pl.CostEstimate(
            flops=2 * sel.size * width, bytes_accessed=2 * rest.shape[0] * width, transcendentals=0
        ),
        name="select_b",
    )(sel, rest)


def weights_kernel(first_row, last, gone, retained, selected, keep, take):
    rows = keep.shape[0]
    label = first_row[0] + lax.broadcasted_iota(jnp.int32, (rows, last.shape[1]), 0)
    is_last, is_gone = label == last[...], label == gone[...]
    kept = jnp.where(is_last, retained[...], jnp.where(is_gone, 0.0, 1.0))
    keep[...] = jnp.min(kept, axis=1, keepdims=True)
    take[...] = jnp.max(jnp.where(is_last, selected[...], 0.0), axis=1, keepdims=True)


def row_weights(first_row, rows, last, gone, retained, selected):
    return pl.pallas_call(
        weights_kernel,
        in_specs=[pl.BlockSpec(memory_space=pltpu.SMEM)] + [VMEM] * 4,
        out_specs=[VMEM] * 2,
        out_shape=[jax.ShapeDtypeStruct((rows, 1), F32)] * 2,
        compiler_params=params(4),
        cost_estimate=pl.CostEstimate(flops=8 * rows * last.shape[0], bytes_accessed=0, transcendentals=0),
        name="row_weights",
    )(first_row[None], last[None, :], gone[None, :], retained[None, :], selected[None, :])


def stack_rows(stack, parts, cols):
    at = 0
    for part in parts:
        stack[at : at + part.shape[0], cols] = part[:, cols]
        at += part.shape[0]


def store_rows(outs, cols, value):
    at = 0
    for out in outs:
        out[:, cols] = value[at : at + out.shape[0]]
        at += out.shape[0]


def turn_kernel(count, *refs):
    sel, parts, outs, stack = refs[0], refs[1 : 1 + count], refs[1 + count : -1], refs[-1]

    def body(cols):
        stack_rows(stack, parts, cols)
        store_rows(outs, cols, jnp.dot(sel[...], stack[:, cols], preferred_element_type=F32).astype(BF))

    tiles(0, stack.shape[1], body)


def turn(sel, parts, counts):
    width = parts[0].shape[1]
    return pl.pallas_call(
        functools.partial(turn_kernel, len(parts)),
        in_specs=[VMEM] * (1 + len(parts)),
        out_specs=[VMEM] * len(counts),
        out_shape=[jax.ShapeDtypeStruct((n, width), BF) for n in counts],
        scratch_shapes=[pltpu.VMEM((sel.shape[1], width), BF)],
        compiler_params=params(8),
        cost_estimate=pl.CostEstimate(
            flops=2 * sel.shape[0] * sel.shape[1] * width, bytes_accessed=sel.size * 2, transcendentals=0
        ),
        name="turn",
    )(sel, *parts)


def blend_kernel(start, main, count, with_side, aliased, *refs):
    place, keep, take, rest = refs[:4]
    ys = refs[4 : 4 + count]
    refs = refs[4 + count :]
    if with_side:
        win, pick = refs[:2]
        refs = refs[2:]
    refs = refs[aliased:]
    if with_side:
        out, mixed, mine, stack, done, sems, edge = refs
    else:
        out, stack, done, sems = refs
    k, t = keep[...], take[...]
    half = stack.shape[1]
    copies = []
    tiles(0, half, lambda cols: stack_rows(stack, ys, cols))
    for q in range(HALVES):
        table = only_half(place[...], q, 1)

        def value(x, at):
            placed = jnp.dot(table, stack[:, pl.ds(at, x.shape[1])], preferred_element_type=F32)
            return (k * x.astype(F32) + t * placed).astype(BF)

        lo, hi = q * half, min((q + 1) * half, main)

        def body(cols, q=q):
            at = pl.multiple_of(cols.start, TILE)
            x = rest[:, pl.ds(pl.multiple_of(start + at, TILE), TILE)]
            done[:, pl.ds(at, TILE)] = value(x, pl.multiple_of(at - q * half, TILE))

        tiles(lo, hi - lo, body)
        copies.append(
            pltpu.make_async_copy(done.at[:, lo:hi], out.at[:, start + lo : start + hi], sems.at[q])
        )
        copies[-1].start()
    if with_side:
        base = main - half
        for at, n in edge_pieces(rest, rest.shape[1] // TILE * TILE):
            x = rest[:, start + main + at : start + main + at + n]
            edge[:, at : at + n] = value(x, base + at)
        copies.append(pltpu.make_async_copy(edge, out.at[:, start + main :], sems.at[HALVES]))
        copies[-1].start()
        for at in range(0, mixed.shape[1], TILE):
            mixed[:, at : at + TILE] = value(win[:, at : at + TILE], base + EDGE + at)
        mine[...] = jnp.dot(mixed[...], pick[...], preferred_element_type=F32).astype(BF)
    for copy in copies:
        copy.wait()


def blend(place, keep, take, ys, rest, start, main, side, into):
    rows, total = rest.shape
    half = ys[0].shape[1]
    with_side, aliased = bool(side), into is not None
    args = [place, keep, take, rest, *ys, *side] + ([into] if aliased else [])
    out_shape, out_specs = [jax.ShapeDtypeStruct((rows, total), BF)], [ANY]
    if with_side:
        out_shape += [jax.ShapeDtypeStruct((rows, n), BF) for n in (side[0].shape[1], side[1].shape[1])]
        out_specs += [VMEM] * 2
    return pl.pallas_call(
        functools.partial(blend_kernel, start, main, len(ys), with_side, aliased),
        in_specs=[VMEM] * (4 + len(ys) + len(side)) + [ANY] * aliased,
        out_specs=out_specs,
        out_shape=out_shape,
        scratch_shapes=[
            pltpu.VMEM((place.shape[1], half), BF),
            pltpu.VMEM((rows, main), BF),
            pltpu.SemaphoreType.DMA((HALVES + 1,)),
        ]
        + ([pltpu.VMEM((rows, total - start - main), BF)] if with_side else []),
        input_output_aliases={len(args) - 1: 0} if aliased else {},
        compiler_params=params(16),
        cost_estimate=pl.CostEstimate(
            flops=4 * place.shape[0] * place.shape[1] * half * HALVES,
            bytes_accessed=2 * rows * half * HALVES,
            transcendentals=0,
        ),
        name="blend",
    )(*args)


def columns_kernel(mixed, keep, take, spread, p0, p1, p2, p3, out, stack, done, sem):
    rows = mixed.shape[0]
    at = 0
    for p in (p0, p1, p2, p3):
        for i in range(p.shape[0] // rows):
            stack[:, at * 128 : (at + 1) * 128] = p[i * rows : (i + 1) * rows, :]
            at += 1

    def body(cols):
        got = jnp.dot(stack[...], spread[:, cols], preferred_element_type=F32)
        done[:, cols] = (keep[:, cols] * mixed[:, cols].astype(F32) + take[:, cols] * got).astype(BF)

    tiles(0, mixed.shape[1], body)
    copy = pltpu.make_async_copy(done, out, sem)
    copy.start()
    copy.wait()


def columns(mixed, keep, take, spread, pieces):
    return pl.pallas_call(
        columns_kernel,
        in_specs=[VMEM] * 8,
        out_specs=ANY,
        out_shape=jax.ShapeDtypeStruct(mixed.shape, BF),
        scratch_shapes=[
            pltpu.VMEM((mixed.shape[0], spread.shape[0]), BF),
            pltpu.VMEM(mixed.shape, BF),
            pltpu.SemaphoreType.DMA,
        ],
        compiler_params=params(8),
        cost_estimate=pl.CostEstimate(
            flops=2 * mixed.size * spread.shape[0], bytes_accessed=2 * mixed.size, transcendentals=0
        ),
        name="columns",
    )(mixed, keep, take, spread, *pieces)


def shards(sim_window, sim_rest, joined_partner_pairs, cluster_member_count):
    rows, wcols = sim_window.shape
    total = sim_rest.shape[1]
    me, my_col = lax.axis_index("row"), lax.axis_index("col")
    cols_n = lax.axis_size("col")
    my_y, my_z = me // NZ, me % NZ
    last, gone = joined_partner_pairs[:, 0], joined_partner_pairs[:, 1]
    src, dst = gone // rows, last // rows
    src_y, src_z, dst_y, dst_z = src // NZ, src % NZ, dst // NZ, dst % NZ
    ahead = (dst_z - src_z) % NZ
    local = jnp.where(src == me, gone - me * rows, -1)
    mine_last = jnp.where(dst == me, last - me * rows, -1)
    to_z = ahead * TO_Z + rank(src * NZ + ahead)
    to_y = (dst_y - src_y) % NY * (NZ * CAP) + src_z * CAP + rank(src * (NY * NZ) + dst)
    list_pos = rank(src)
    in_line = jnp.where((src_z == my_z) & (dst_y == my_y), (my_y - src_y) % NY * SEND + list_pos, -1)
    to_z_b = ahead * TO_Z + rank(src_z * (NY * NZ) + dst)
    two = lambda n: (n, HALVES)
    one = lambda n: (n, 1)
    (sel_a,) = joins((two(SLOTS), to_z, one(rows), local))
    (sel_b,) = joins((two(SEND), list_pos, one(rows), local))
    turn_b, turn_a, place_a, place_b = joins(
        (two(SLOTS), to_z_b, two(SLOTS), in_line),
        (two(SLOTS), to_y, two(SLOTS), jnp.where((src_y == my_y) & (dst_z == my_z), to_z, -1)),
        (one(rows), mine_last, two(SLOTS), to_y),
        (one(rows), mine_last, two(SLOTS), to_z_b),
    )

    counts2d = cluster_member_count.astype(BF).reshape(-1, 128)
    size_last, size_gone = sizes_of(last, counts2d), sizes_of(gone, counts2d)
    retained, selected = size_last / (size_last + size_gone), size_gone / (size_last + size_gone)
    keep, take = row_weights(me * rows, rows, last, gone, retained, selected)
    gone_col = gone // wcols
    col_rank = rank(gone_col)
    lane = 128
    pick = join(hot(gone - my_col * wcols, wcols), hot(col_rank, lane, gone_col == my_col))

    whole = total // TILE * TILE

    def across(lists, along_z):
        got = list(lists)
        for d in Z_ORDER if along_z else Y_ORDER:
            got[d] = lax.ppermute(lists[d], "row", row_perm(0, d) if along_z else row_perm(d, 0))
        return got

    z_counts, y_counts = (TO_Z * HALVES,) * NZ, (SEND * HALVES,) * NY
    lists_a = select_a(sel_a, z_counts, sim_rest, sim_window, SPLIT, whole - SPLIT)
    list_b = select_b(sel_b, sim_rest, SPLIT)
    got_a = across(lists_a, True)
    got_b = across([list_b] * NY, False)
    got_b = across(turn(turn_b, got_b, z_counts), True)
    turned_a = turn(turn_a, got_a, y_counts)
    got_a = across(turned_a, False)

    into, mixed, mine = blend(
        place_a, keep, take, got_a, sim_rest, SPLIT, whole - SPLIT, (sim_window, pick), None
    )
    (rest_out,) = blend(place_b, keep, take, got_b, sim_rest, 0, SPLIT, (), into)

    pieces = [mine]
    step = 1
    while step < cols_n:
        so_far = jnp.concatenate(pieces, axis=0)
        pieces.append(lax.ppermute(so_far, "col", [(c, c ^ step) for c in range(cols_n)]))
        step *= 2
    spread = join(
        hot((my_col ^ gone_col) * lane + col_rank, cols_n * lane), hot(last - my_col * wcols, wcols)
    )
    ckeep, ctake = item_weights(
        my_col * wcols + jnp.arange(wcols, dtype=jnp.int32), last, gone, retained, selected
    )
    window_out = columns(mixed, ckeep[None, :], ctake[None, :], spread, pieces)
    return window_out, rest_out


def solution(mesh):
    in_specs = (P("row", "col"), P("row", "col"), P(), P())
    out_specs = (P("row", "col"), P("row", "col"))

    return jax.shard_map(shards, mesh=mesh, in_specs=in_specs, out_specs=out_specs, check_vma=False)
```

profile of v0, /device:TPU:1, one launch (start us, length us, event | category | flops | bytes accessed | tf_op | source)
XLA Modules:
  0.0 132.9 jit_solution(2618455057074628170)
XLA Ops:
  0.7 0.9 and_select_fusion.12
  1.5 0.7 compare_select_fusion.18
  2.7 0.8 and_select_fusion.5
  3.8 1.0 copy-done.1
  4.8 3.2 %select_a.1 = (bf16[24,3840]{1,0:T(8,128)(2,1)S(1)}, bf16[24,3840]{1,0:T(8,128)(2,1)S(1)}, bf16[24,3840]{1,0:T(8,128)(2,1)S(1)}, bf16[24,3840]{1,0:T(8,128)(2,1)...) custom-call(bf16[192,192]{1,0:T(8,128)(2,1)S(1)} %shard_map.60.refs_, ...), custom_call_target="tpu_custom_call" | custom-call | flops 566231040 | bytes 2949120 | tf_op jit(solution)/shard_map/select_a/pallas_call | solution.py:158
  8.0 2.5 %collective-permute-start = (bf16[24,3840]{1,0:T(8,128)(2,1)S(1)}, bf16[24,3840]{1,0:T(8,128)(2,1)S(1)}, u32[]{:S(2)}, u32[]{:S(2)}) collective-permute-start(bf16[24,3840]{1,0:T(8,128)(2,1)S(1)} %get-tuple-element.36), channel_id=1, source_target_pairs={{0,8},{8,16},{16,24},{24,32},{32,40},{40,48},{48,56},{56,0},{64,72... | collective-permute-start | bytes 552968 | tf_op jit(solution)/shard_map/ppermute | solution.py:414
  10.5 3.0 %collective-permute-start.1 = (bf16[24,3840]{1,0:T(8,128)(2,1)S(1)}, bf16[24,3840]{1,0:T(8,128)(2,1)S(1)}, u32[]{:S(2)}, u32[]{:S(2)}) collective-permute-start(bf16[24,3840]{1,0:T(8,128)(2,1)S(1)} %get-tuple-element.37), channel_id=1, source_target_pairs={{0,16},{8,24},{16,32},{24,40},{32,48},{40,56},{48,0},{56,8},{64,80... | collective-permute-start | bytes 552968 | tf_op jit(solution)/shard_map/ppermute | solution.py:414
  13.5 3.8 %collective-permute-start.2 = (bf16[24,3840]{1,0:T(8,128)(2,1)S(1)}, bf16[24,3840]{1,0:T(8,128)(2,1)S(1)}, u32[]{:S(2)}, u32[]{:S(2)}) collective-permute-start(bf16[24,3840]{1,0:T(8,128)(2,1)S(1)} %get-tuple-element.38), channel_id=1, source_target_pairs={{0,24},{8,32},{16,40},{24,48},{32,56},{40,0},{48,8},{56,16},{64,88... | collective-permute-start | bytes 552968 | tf_op jit(solution)/shard_map/ppermute | solution.py:414
  17.2 0.5 collective-permute-start.3
  17.7 4.5 %collective-permute-start.4 = (bf16[24,3840]{1,0:T(8,128)(2,1)S(1)}, bf16[24,3840]{1,0:T(8,128)(2,1)S(1)}, u32[]{:S(2)}, u32[]{:S(2)}) collective-permute-start(bf16[24,3840]{1,0:T(8,128)(2,1)S(1)} %get-tuple-element.40), channel_id=1, source_target_pairs={{0,40},{8,48},{16,56},{24,0},{32,8},{40,16},{48,24},{56,32},{64,10... | collective-permute-start | bytes 552968 | tf_op jit(solution)/shard_map/ppermute | solution.py:414
  22.8 0.9 select_b.1.refs_1_
  24.5 0.4 convert_reduce_fusion.5
  25.0 0.5 shard_map.59
  25.5 2.5 %collective-permute-start.5 = (bf16[24,3840]{1,0:T(8,128)(2,1)S(1)}, bf16[24,3840]{1,0:T(8,128)(2,1)S(1)}, u32[]{:S(2)}, u32[]{:S(2)}) collective-permute-start(bf16[24,3840]{1,0:T(8,128)(2,1)S(1)} %get-tuple-element.41), channel_id=1, source_target_pairs={{0,48},{8,56},{16,0},{24,8},{32,16},{40,24},{48,32},{56,40},{64,11... | collective-permute-start | bytes 552968 | tf_op jit(solution)/shard_map/ppermute | solution.py:414
  28.0 1.3 %collective-permute-start.6 = (bf16[24,3840]{1,0:T(8,128)(2,1)S(1)}, bf16[24,3840]{1,0:T(8,128)(2,1)S(1)}, u32[]{:S(2)}, u32[]{:S(2)}) collective-permute-start(bf16[24,3840]{1,0:T(8,128)(2,1)S(1)} %get-tuple-element.42), channel_id=1, source_target_pairs={{0,56},{8,0},{16,8},{24,16},{32,24},{40,32},{48,40},{56,48},{64,12... | collective-permute-start | bytes 552968 | tf_op jit(solution)/shard_map/ppermute | solution.py:414
  29.3 1.7 %fusion.9.spread = bf16[1024,768]{1,0:T(8,128)(2,1)S(1)} fusion(s32[768]{0:T(1024)S(1)} %multiply_add_fusion, s32[768]{0:T(1024)S(1)} %get-tuple-element.105), kind=kOutput, calls=%fused_computation.22 | convolution fusion | flops 1210122240 | bytes 1579008 | tf_op jit(solution)/shard_map/dot_general | solution.py:43
  31.0 6.8 %collective-permute-done.2.refs_4_ = bf16[24,3840]{1,0:T(8,128)(2,1)S(1)} collective-permute-done((bf16[24,3840]{1,0:T(8,128)(2,1)S(1)}, bf16[24,3840]{1,0:T(8,128)(2,1)S(1)}, u32[]{:S(2)}, u32[]{:S(2)}) %collective-permute-start.2) | collective-permute-done | bytes 184352 | tf_op jit(solution)/shard_map/ppermute | solution.py:414
  37.9 2.7 %collective-permute-start.15 = (bf16[48,3840]{1,0:T(8,128)(2,1)S(1)}, bf16[48,3840]{1,0:T(8,128)(2,1)S(1)}, u32[]{:S(2)}, u32[]{:S(2)}) collective-permute-start(bf16[48,3840]{1,0:T(8,128)(2,1)S(1)} %select_b.1.refs_1_), channel_id=1, source_target_pairs={{0,192},{8,200},{16,208},{24,216},{32,224},{40,232},{48,240},{56,2... | collective-permute-start | bytes 1105928 | tf_op jit(solution)/shard_map/ppermute | solution.py:414
  40.6 1.6 %collective-permute-done.3.refs_5_ = bf16[24,3840]{1,0:T(8,128)(2,1)S(1)} collective-permute-done((bf16[24,3840]{1,0:T(8,128)(2,1)S(1)}, bf16[24,3840]{1,0:T(8,128)(2,1)S(1)}, u32[]{:S(2)}, u32[]{:S(2)}) %collective-permute-start.3) | collective-permute-done | bytes 184352 | tf_op jit(solution)/shard_map/ppermute | solution.py:414
  42.2 2.9 %collective-permute-start.14 = (bf16[48,3840]{1,0:T(8,128)(2,1)S(1)}, bf16[48,3840]{1,0:T(8,128)(2,1)S(1)}, u32[]{:S(2)}, u32[]{:S(2)}) collective-permute-start(bf16[48,3840]{1,0:T(8,128)(2,1)S(1)} %select_b.1.refs_1_), channel_id=1, source_target_pairs={{0,128},{8,136},{16,144},{24,152},{32,160},{40,168},{48,176},{56,1... | collective-permute-start | bytes 1105928 | tf_op jit(solution)/shard_map/ppermute | solution.py:414
  45.1 5.1 %collective-permute-done.5.refs_7_ = bf16[24,3840]{1,0:T(8,128)(2,1)S(1)} collective-permute-done((bf16[24,3840]{1,0:T(8,128)(2,1)S(1)}, bf16[24,3840]{1,0:T(8,128)(2,1)S(1)}, u32[]{:S(2)}, u32[]{:S(2)}) %collective-permute-start.5) | collective-permute-done | bytes 184352 | tf_op jit(solution)/shard_map/ppermute | solution.py:414
  50.2 1.0 collective-permute-done.6.refs_8_
  51.2 0.9 turn.2
  52.1 1.5 %collective-permute-start.7 = (bf16[48,3840]{1,0:T(8,128)(2,1)S(1)}, bf16[48,3840]{1,0:T(8,128)(2,1)S(1)}, u32[]{:S(2)}, u32[]{:S(2)}) collective-permute-start(bf16[48,3840]{1,0:T(8,128)(2,1)S(1)} %get-tuple-element.44), channel_id=1, source_target_pairs={{0,64},{8,72},{16,80},{24,88},{32,96},{40,104},{48,112},{56,120},{... | collective-permute-start | bytes 1105928 | tf_op jit(solution)/shard_map/ppermute | solution.py:414
  53.9 2.7 %collective-permute-start.8 = (bf16[48,3840]{1,0:T(8,128)(2,1)S(1)}, bf16[48,3840]{1,0:T(8,128)(2,1)S(1)}, u32[]{:S(2)}, u32[]{:S(2)}) collective-permute-start(bf16[48,3840]{1,0:T(8,128)(2,1)S(1)} %get-tuple-element.45), channel_id=1, source_target_pairs={{0,128},{8,136},{16,144},{24,152},{32,160},{40,168},{48,176},{56,1... | collective-permute-start | bytes 1105928 | tf_op jit(solution)/shard_map/ppermute | solution.py:414
  56.7 1.1 collective-permute-start.9
  58.0 0.6 fusion.13.refs_9_
  58.6 4.1 %collective-permute-done.7.refs_5_ = bf16[48,3840]{1,0:T(8,128)(2,1)S(1)} collective-permute-done((bf16[48,3840]{1,0:T(8,128)(2,1)S(1)}, bf16[48,3840]{1,0:T(8,128)(2,1)S(1)}, u32[]{:S(2)}, u32[]{:S(2)}) %collective-permute-start.7) | collective-permute-done | bytes 368672 | tf_op jit(solution)/shard_map/ppermute | solution.py:414
  62.9 8.8 %collective-permute-done.8.refs_6_ = bf16[48,3840]{1,0:T(8,128)(2,1)S(1)} collective-permute-done((bf16[48,3840]{1,0:T(8,128)(2,1)S(1)}, bf16[48,3840]{1,0:T(8,128)(2,1)S(1)}, u32[]{:S(2)}, u32[]{:S(2)}) %collective-permute-start.8) | collective-permute-done | bytes 368672 | tf_op jit(solution)/shard_map/ppermute | solution.py:414
  71.7 1.8 %collective-permute-done.9.refs_7_ = bf16[48,3840]{1,0:T(8,128)(2,1)S(1)} collective-permute-done((bf16[48,3840]{1,0:T(8,128)(2,1)S(1)}, bf16[48,3840]{1,0:T(8,128)(2,1)S(1)}, u32[]{:S(2)}, u32[]{:S(2)}) %collective-permute-start.9) | collective-permute-done | bytes 368672 | tf_op jit(solution)/shard_map/ppermute | solution.py:414
  73.5 3.3 %blend.2 = (bf16[192,14232]{1,0:T(8,128)(2,1)}, bf16[192,768]{1,0:T(8,128)(2,1)S(1)}, bf16[192,128]{1,0:T(8,128)(2,1)S(1)}) custom-call(bf16[192,192]{1,0:T(8,128)(2,1)S(1)} %get-tuple-element.31.refs_0_, f32[192,1]{1,0:T(8,128)S(1)} %get-tuple-element.32.refs_1_, f32[192,1]{1,0:T(8,128)S(1)} %get-tuple-element.33.refs_2_, bf16[192,14232]{1,0:T(8,128)(2,1)S(1)} %copy-done, ...), custom_call_target="tpu_custom_call" | custom-call | flops 1132462080 | bytes 2949120 | tf_op jit(solution)/shard_map/blend/pallas_call | solution.py:313
  76.8 2.1 %collective-permute-start.10 = (bf16[192,128]{1,0:T(8,128)(2,1)S(1)}, bf16[192,128]{1,0:T(8,128)(2,1)S(1)}, u32[]{:S(2)}, u32[]{:S(2)}) collective-permute-start(bf16[192,128]{1,0:T(8,128)(2,1)S(1)} %get-tuple-element.48.p0), channel_id=1, source_target_pairs={{0,1},{1,0},{2,3},{3,2},{4,5},{5,4},{6,7},{7,6},{8,9},{9,8},{10,11... | collective-permute-start | bytes 147464 | tf_op jit(solution)/shard_map/ppermute | solution.py:435
  78.9 1.7 %collective-permute-done.13.refs_2_ = bf16[48,3840]{1,0:T(8,128)(2,1)S(1)} collective-permute-done((bf16[48,3840]{1,0:T(8,128)(2,1)S(1)}, bf16[48,3840]{1,0:T(8,128)(2,1)S(1)}, u32[]{:S(2)}, u32[]{:S(2)}) %collective-permute-start.13) | collective-permute-done | bytes 368672 | tf_op jit(solution)/shard_map/ppermute | solution.py:414
  80.5 0.9 turn.3
  81.4 4.7 %collective-permute-start.16 = (bf16[24,3840]{1,0:T(8,128)(2,1)S(1)}, bf16[24,3840]{1,0:T(8,128)(2,1)S(1)}, u32[]{:S(2)}, u32[]{:S(2)}) collective-permute-start(bf16[24,3840]{1,0:T(8,128)(2,1)S(1)} %get-tuple-element.52), channel_id=1, source_target_pairs={{0,8},{8,16},{16,24},{24,32},{32,40},{40,48},{48,56},{56,0},{64,72... | collective-permute-start | bytes 552968 | tf_op jit(solution)/shard_map/ppermute | solution.py:414
  86.1 0.8 collective-permute-start.17
  87.0 5.2 %collective-permute-start.18 = (bf16[24,3840]{1,0:T(8,128)(2,1)S(1)}, bf16[24,3840]{1,0:T(8,128)(2,1)S(1)}, u32[]{:S(2)}, u32[]{:S(2)}) collective-permute-start(bf16[24,3840]{1,0:T(8,128)(2,1)S(1)} %get-tuple-element.54), channel_id=1, source_target_pairs={{0,24},{8,32},{16,40},{24,48},{32,56},{40,0},{48,8},{56,16},{64,88... | collective-permute-start | bytes 552968 | tf_op jit(solution)/shard_map/ppermute | solution.py:414
  92.1 1.3 collective-permute-start.11
  93.4 1.0 fusion.2
  94.5 1.5 %collective-permute-done.11.p2 = bf16[384,128]{1,0:T(8,128)(2,1)S(1)} collective-permute-done((bf16[384,128]{1,0:T(8,128)(2,1)S(1)}, bf16[384,128]{1,0:T(8,128)(2,1)S(1)}, u32[]{:S(2)}, u32[]{:S(2)}) %collective-permute-start.11) | collective-permute-done | bytes 98336 | tf_op jit(solution)/shard_map/ppermute | solution.py:435
  96.0 2.8 %collective-permute-start.20 = (bf16[24,3840]{1,0:T(8,128)(2,1)S(1)}, bf16[24,3840]{1,0:T(8,128)(2,1)S(1)}, u32[]{:S(2)}, u32[]{:S(2)}) collective-permute-start(bf16[24,3840]{1,0:T(8,128)(2,1)S(1)} %get-tuple-element.56), channel_id=1, source_target_pairs={{0,40},{8,48},{16,56},{24,0},{32,8},{40,16},{48,24},{56,32},{64,10... | collective-permute-start | bytes 552968 | tf_op jit(solution)/shard_map/ppermute | solution.py:414
  98.9 0.5 collective-permute-done.17.refs_6_
  99.5 8.7 %collective-permute-start.22 = (bf16[24,3840]{1,0:T(8,128)(2,1)S(1)}, bf16[24,3840]{1,0:T(8,128)(2,1)S(1)}, u32[]{:S(2)}, u32[]{:S(2)}) collective-permute-start(bf16[24,3840]{1,0:T(8,128)(2,1)S(1)} %get-tuple-element.58), channel_id=1, source_target_pairs={{0,56},{8,0},{16,8},{24,16},{32,24},{40,32},{48,40},{56,48},{64,12... | collective-permute-start | bytes 552968 | tf_op jit(solution)/shard_map/ppermute | solution.py:414
  108.2 14.7 %collective-permute-done.18.refs_7_ = bf16[24,3840]{1,0:T(8,128)(2,1)S(1)} collective-permute-done((bf16[24,3840]{1,0:T(8,128)(2,1)S(1)}, bf16[24,3840]{1,0:T(8,128)(2,1)S(1)}, u32[]{:S(2)}, u32[]{:S(2)}) %collective-permute-start.18) | collective-permute-done | bytes 184352 | tf_op jit(solution)/shard_map/ppermute | solution.py:414
  122.8 2.8 %collective-permute-start.12 = (bf16[768,128]{1,0:T(8,128)(2,1)S(1)}, bf16[768,128]{1,0:T(8,128)(2,1)S(1)}, u32[]{:S(2)}, u32[]{:S(2)}) collective-permute-start(bf16[768,128]{1,0:T(8,128)(2,1)S(1)} %pad_maximum_fusion), channel_id=1, source_target_pairs={{0,4},{1,5},{2,6},{3,7},{4,0},{5,1},{6,2},{7,3},{8,12},{9,13},{10,... | collective-permute-start | bytes 589832 | tf_op jit(solution)/shard_map/ppermute | solution.py:435
  125.6 2.1 %collective-permute-done.22.refs_11_ = bf16[24,3840]{1,0:T(8,128)(2,1)S(1)} collective-permute-done((bf16[24,3840]{1,0:T(8,128)(2,1)S(1)}, bf16[24,3840]{1,0:T(8,128)(2,1)S(1)}, u32[]{:S(2)}, u32[]{:S(2)}) %collective-permute-start.22) | collective-permute-done | bytes 184352 | tf_op jit(solution)/shard_map/ppermute | solution.py:414
  127.8 3.7 %blend.3 = bf16[192,14232]{1,0:T(8,128)(2,1)} custom-call(bf16[192,192]{1,0:T(8,128)(2,1)S(1)} %get-tuple-element.49.refs_0_, f32[192,1]{1,0:T(8,128)S(1)} %get-tuple-element.32.refs_1_, f32[192,1]{1,0:T(8,128)S(1)} %get-tuple-element.33.refs_2_, bf16[192,14232]{1,0:T(8,128)(2,1)S(1)} %copy-done, ...), custom_call_target="tpu_custom_call", output_to_operand_aliasing={{}: (12, {})} | custom-call | flops 1132462080 | bytes 2949120 | tf_op jit(solution)/shard_map/blend/pallas_call | solution.py:313
  131.5 1.2 columns.1
  (45 shorter events, 3.2 us)
Async XLA Ops:
  3.8 1.0 copy-start.1
  4.8 18.0 %copy-start = (bf16[192,14232]{1,0:T(8,128)(2,1)S(1)}, bf16[192,14232]{1,0:T(8,128)(2,1)}, u32[]{:S(2)}) copy-start(bf16[192,14232]{1,0:T(8,128)(2,1)} %refs_3_.3) | copy-start | bytes 16395268
  8.0 17.6 %collective-permute-start = (bf16[24,3840]{1,0:T(8,128)(2,1)S(1)}, bf16[24,3840]{1,0:T(8,128)(2,1)S(1)}, u32[]{:S(2)}, u32[]{:S(2)}) collective-permute-start(bf16[24,3840]{1,0:T(8,128)(2,1)S(1)} %get-tuple-element.36), channel_id=1, source_target_pairs={{0,8},{8,16},{16,24},{24,32},{32,40},{40,48},{48,56},{56,0},{64,72... | collective-permute-start | bytes 552968 | tf_op jit(solution)/shard_map/ppermute | solution.py:414
  10.5 17.5 %collective-permute-start.1 = (bf16[24,3840]{1,0:T(8,128)(2,1)S(1)}, bf16[24,3840]{1,0:T(8,128)(2,1)S(1)}, u32[]{:S(2)}, u32[]{:S(2)}) collective-permute-start(bf16[24,3840]{1,0:T(8,128)(2,1)S(1)} %get-tuple-element.37), channel_id=1, source_target_pairs={{0,16},{8,24},{16,32},{24,40},{32,48},{40,56},{48,0},{56,8},{64,80... | collective-permute-start | bytes 552968 | tf_op jit(solution)/shard_map/ppermute | solution.py:414
  13.5 24.4 %collective-permute-start.2 = (bf16[24,3840]{1,0:T(8,128)(2,1)S(1)}, bf16[24,3840]{1,0:T(8,128)(2,1)S(1)}, u32[]{:S(2)}, u32[]{:S(2)}) collective-permute-start(bf16[24,3840]{1,0:T(8,128)(2,1)S(1)} %get-tuple-element.38), channel_id=1, source_target_pairs={{0,24},{8,32},{16,40},{24,48},{32,56},{40,0},{48,8},{56,16},{64,88... | collective-permute-start | bytes 552968 | tf_op jit(solution)/shard_map/ppermute | solution.py:414
  17.2 24.9 %collective-permute-start.3 = (bf16[24,3840]{1,0:T(8,128)(2,1)S(1)}, bf16[24,3840]{1,0:T(8,128)(2,1)S(1)}, u32[]{:S(2)}, u32[]{:S(2)}) collective-permute-start(bf16[24,3840]{1,0:T(8,128)(2,1)S(1)} %get-tuple-element.39), channel_id=1, source_target_pairs={{0,32},{8,40},{16,48},{24,56},{32,0},{40,8},{48,16},{56,24},{64,96... | collective-permute-start | bytes 552968 | tf_op jit(solution)/shard_map/ppermute | solution.py:414
  17.7 27.4 %collective-permute-start.4 = (bf16[24,3840]{1,0:T(8,128)(2,1)S(1)}, bf16[24,3840]{1,0:T(8,128)(2,1)S(1)}, u32[]{:S(2)}, u32[]{:S(2)}) collective-permute-start(bf16[24,3840]{1,0:T(8,128)(2,1)S(1)} %get-tuple-element.40), channel_id=1, source_target_pairs={{0,40},{8,48},{16,56},{24,0},{32,8},{40,16},{48,24},{56,32},{64,10... | collective-permute-start | bytes 552968 | tf_op jit(solution)/shard_map/ppermute | solution.py:414
  22.8 2.0 %copy-start.2 = (s32[768,2]{0,1:T(2,128)S(1)}, s32[768,2]{0,1:T(2,128)}, u32[]{:S(2)}) copy-start(s32[768,2]{0,1:T(2,128)} %param.6) | copy-start | bytes 18436
  25.5 24.6 %collective-permute-start.5 = (bf16[24,3840]{1,0:T(8,128)(2,1)S(1)}, bf16[24,3840]{1,0:T(8,128)(2,1)S(1)}, u32[]{:S(2)}, u32[]{:S(2)}) collective-permute-start(bf16[24,3840]{1,0:T(8,128)(2,1)S(1)} %get-tuple-element.41), channel_id=1, source_target_pairs={{0,48},{8,56},{16,0},{24,8},{32,16},{40,24},{48,32},{56,40},{64,11... | collective-permute-start | bytes 552968 | tf_op jit(solution)/shard_map/ppermute | solution.py:414
  28.0 23.2 %collective-permute-start.6 = (bf16[24,3840]{1,0:T(8,128)(2,1)S(1)}, bf16[24,3840]{1,0:T(8,128)(2,1)S(1)}, u32[]{:S(2)}, u32[]{:S(2)}) collective-permute-start(bf16[24,3840]{1,0:T(8,128)(2,1)S(1)} %get-tuple-element.42), channel_id=1, source_target_pairs={{0,56},{8,0},{16,8},{24,16},{32,24},{40,32},{48,40},{56,48},{64,12... | collective-permute-start | bytes 552968 | tf_op jit(solution)/shard_map/ppermute | solution.py:414
  29.3 24.3 %copy-start.3 = (s32[6144]{0:T(1024)S(1)}, s32[6144]{0:T(1024)}, u32[]{:S(2)}) copy-start(s32[6144]{0:T(1024)} %param.7) | copy-start | bytes 73732
  37.9 41.0 %collective-permute-start.15 = (bf16[48,3840]{1,0:T(8,128)(2,1)S(1)}, bf16[48,3840]{1,0:T(8,128)(2,1)S(1)}, u32[]{:S(2)}, u32[]{:S(2)}) collective-permute-start(bf16[48,3840]{1,0:T(8,128)(2,1)S(1)} %select_b.1.refs_1_), channel_id=1, source_target_pairs={{0,192},{8,200},{16,208},{24,216},{32,224},{40,232},{48,240},{56,2... | collective-permute-start | bytes 1105928 | tf_op jit(solution)/shard_map/ppermute | solution.py:414
  42.2 36.7 %collective-permute-start.14 = (bf16[48,3840]{1,0:T(8,128)(2,1)S(1)}, bf16[48,3840]{1,0:T(8,128)(2,1)S(1)}, u32[]{:S(2)}, u32[]{:S(2)}) collective-permute-start(bf16[48,3840]{1,0:T(8,128)(2,1)S(1)} %select_b.1.refs_1_), channel_id=1, source_target_pairs={{0,128},{8,136},{16,144},{24,152},{32,160},{40,168},{48,176},{56,1... | collective-permute-start | bytes 1105928 | tf_op jit(solution)/shard_map/ppermute | solution.py:414
  52.1 10.5 %collective-permute-start.7 = (bf16[48,3840]{1,0:T(8,128)(2,1)S(1)}, bf16[48,3840]{1,0:T(8,128)(2,1)S(1)}, u32[]{:S(2)}, u32[]{:S(2)}) collective-permute-start(bf16[48,3840]{1,0:T(8,128)(2,1)S(1)} %get-tuple-element.44), channel_id=1, source_target_pairs={{0,64},{8,72},{16,80},{24,88},{32,96},{40,104},{48,112},{56,120},{... | collective-permute-start | bytes 1105928 | tf_op jit(solution)/shard_map/ppermute | solution.py:414
  53.9 17.7 %collective-permute-start.8 = (bf16[48,3840]{1,0:T(8,128)(2,1)S(1)}, bf16[48,3840]{1,0:T(8,128)(2,1)S(1)}, u32[]{:S(2)}, u32[]{:S(2)}) collective-permute-start(bf16[48,3840]{1,0:T(8,128)(2,1)S(1)} %get-tuple-element.45), channel_id=1, source_target_pairs={{0,128},{8,136},{16,144},{24,152},{32,160},{40,168},{48,176},{56,1... | collective-permute-start | bytes 1105928 | tf_op jit(solution)/shard_map/ppermute | solution.py:414
  56.7 16.8 %collective-permute-start.9 = (bf16[48,3840]{1,0:T(8,128)(2,1)S(1)}, bf16[48,3840]{1,0:T(8,128)(2,1)S(1)}, u32[]{:S(2)}, u32[]{:S(2)}) collective-permute-start(bf16[48,3840]{1,0:T(8,128)(2,1)S(1)} %get-tuple-element.46), channel_id=1, source_target_pairs={{0,192},{8,200},{16,208},{24,216},{32,224},{40,232},{48,240},{56,2... | collective-permute-start | bytes 1105928 | tf_op jit(solution)/shard_map/ppermute | solution.py:414
  62.6 17.9 %collective-permute-start.13 = (bf16[48,3840]{1,0:T(8,128)(2,1)S(1)}, bf16[48,3840]{1,0:T(8,128)(2,1)S(1)}, u32[]{:S(2)}, u32[]{:S(2)}) collective-permute-start(bf16[48,3840]{1,0:T(8,128)(2,1)S(1)} %select_b.1.refs_1_), channel_id=1, source_target_pairs={{0,64},{8,72},{16,80},{24,88},{32,96},{40,104},{48,112},{56,120},{... | collective-permute-start | bytes 1105928 | tf_op jit(solution)/shard_map/ppermute | solution.py:414
  76.8 15.4 %collective-permute-start.10 = (bf16[192,128]{1,0:T(8,128)(2,1)S(1)}, bf16[192,128]{1,0:T(8,128)(2,1)S(1)}, u32[]{:S(2)}, u32[]{:S(2)}) collective-permute-start(bf16[192,128]{1,0:T(8,128)(2,1)S(1)} %get-tuple-element.48.p0), channel_id=1, source_target_pairs={{0,1},{1,0},{2,3},{3,2},{4,5},{5,4},{6,7},{7,6},{8,9},{9,8},{10,11... | collective-permute-start | bytes 147464 | tf_op jit(solution)/shard_map/ppermute | solution.py:435
  81.4 17.4 %collective-permute-start.16 = (bf16[24,3840]{1,0:T(8,128)(2,1)S(1)}, bf16[24,3840]{1,0:T(8,128)(2,1)S(1)}, u32[]{:S(2)}, u32[]{:S(2)}) collective-permute-start(bf16[24,3840]{1,0:T(8,128)(2,1)S(1)} %get-tuple-element.52), channel_id=1, source_target_pairs={{0,8},{8,16},{16,24},{24,32},{32,40},{40,48},{48,56},{56,0},{64,72... | collective-permute-start | bytes 552968 | tf_op jit(solution)/shard_map/ppermute | solution.py:414
  86.1 13.3 %collective-permute-start.17 = (bf16[24,3840]{1,0:T(8,128)(2,1)S(1)}, bf16[24,3840]{1,0:T(8,128)(2,1)S(1)}, u32[]{:S(2)}, u32[]{:S(2)}) collective-permute-start(bf16[24,3840]{1,0:T(8,128)(2,1)S(1)} %get-tuple-element.53), channel_id=1, source_target_pairs={{0,16},{8,24},{16,32},{24,40},{32,48},{40,56},{48,0},{56,8},{64,80... | collective-permute-start | bytes 552968 | tf_op jit(solution)/shard_map/ppermute | solution.py:414
  87.0 35.9 %collective-permute-start.18 = (bf16[24,3840]{1,0:T(8,128)(2,1)S(1)}, bf16[24,3840]{1,0:T(8,128)(2,1)S(1)}, u32[]{:S(2)}, u32[]{:S(2)}) collective-permute-start(bf16[24,3840]{1,0:T(8,128)(2,1)S(1)} %get-tuple-element.54), channel_id=1, source_target_pairs={{0,24},{8,32},{16,40},{24,48},{32,56},{40,0},{48,8},{56,16},{64,88... | collective-permute-start | bytes 552968 | tf_op jit(solution)/shard_map/ppermute | solution.py:414
  92.1 3.8 %collective-permute-start.11 = (bf16[384,128]{1,0:T(8,128)(2,1)S(1)}, bf16[384,128]{1,0:T(8,128)(2,1)S(1)}, u32[]{:S(2)}, u32[]{:S(2)}) collective-permute-start(bf16[384,128]{1,0:T(8,128)(2,1)S(1)} %pad_maximum_fusion.1), channel_id=1, source_target_pairs={{0,2},{1,3},{2,0},{3,1},{4,6},{5,7},{6,4},{7,5},{8,10},{9,11},{10,... | collective-permute-start | bytes 294920 | tf_op jit(solution)/shard_map/ppermute | solution.py:435
  94.4 31.2 %collective-permute-start.19 = (bf16[24,3840]{1,0:T(8,128)(2,1)S(1)}, bf16[24,3840]{1,0:T(8,128)(2,1)S(1)}, u32[]{:S(2)}, u32[]{:S(2)}) collective-permute-start(bf16[24,3840]{1,0:T(8,128)(2,1)S(1)} %get-tuple-element.55), channel_id=1, source_target_pairs={{0,32},{8,40},{16,48},{24,56},{32,0},{40,8},{48,16},{56,24},{64,96... | collective-permute-start | bytes 552968 | tf_op jit(solution)/shard_map/ppermute | solution.py:414
  96.0 29.6 %collective-permute-start.20 = (bf16[24,3840]{1,0:T(8,128)(2,1)S(1)}, bf16[24,3840]{1,0:T(8,128)(2,1)S(1)}, u32[]{:S(2)}, u32[]{:S(2)}) collective-permute-start(bf16[24,3840]{1,0:T(8,128)(2,1)S(1)} %get-tuple-element.56), channel_id=1, source_target_pairs={{0,40},{8,48},{16,56},{24,0},{32,8},{40,16},{48,24},{56,32},{64,10... | collective-permute-start | bytes 552968 | tf_op jit(solution)/shard_map/ppermute | solution.py:414
  98.8 26.8 %collective-permute-start.21 = (bf16[24,3840]{1,0:T(8,128)(2,1)S(1)}, bf16[24,3840]{1,0:T(8,128)(2,1)S(1)}, u32[]{:S(2)}, u32[]{:S(2)}) collective-permute-start(bf16[24,3840]{1,0:T(8,128)(2,1)S(1)} %get-tuple-element.57), channel_id=1, source_target_pairs={{0,48},{8,56},{16,0},{24,8},{32,16},{40,24},{48,32},{56,40},{64,11... | collective-permute-start | bytes 552968 | tf_op jit(solution)/shard_map/ppermute | solution.py:414
  99.5 28.3 %collective-permute-start.22 = (bf16[24,3840]{1,0:T(8,128)(2,1)S(1)}, bf16[24,3840]{1,0:T(8,128)(2,1)S(1)}, u32[]{:S(2)}, u32[]{:S(2)}) collective-permute-start(bf16[24,3840]{1,0:T(8,128)(2,1)S(1)} %get-tuple-element.58), channel_id=1, source_target_pairs={{0,56},{8,0},{16,8},{24,16},{32,24},{40,32},{48,40},{56,48},{64,12... | collective-permute-start | bytes 552968 | tf_op jit(solution)/shard_map/ppermute | solution.py:414
  122.8 8.6 %collective-permute-start.12 = (bf16[768,128]{1,0:T(8,128)(2,1)S(1)}, bf16[768,128]{1,0:T(8,128)(2,1)S(1)}, u32[]{:S(2)}, u32[]{:S(2)}) collective-permute-start(bf16[768,128]{1,0:T(8,128)(2,1)S(1)} %pad_maximum_fusion), channel_id=1, source_target_pairs={{0,4},{1,5},{2,6},{3,7},{4,0},{5,1},{6,2},{7,3},{8,12},{9,13},{10,... | collective-permute-start | bytes 589832 | tf_op jit(solution)/shard_map/ppermute | solution.py:435
where the time goes:
time: 134 us; the launch traced here: 133 us
  starting transfers between devices  57.5 us (43%)
  waiting for transfers between devices  49.6 us (37%)
  Pallas kernels  15.3 us (11%)
  other arithmetic  5.39 us (4%)
  matrix products  2.79 us (2%)
    ppermute x20, starting transfers between devices, across(): lax.ppermute(lists[d], 'row', row_perm(0, d) if along_z else row_perm(d, 0))  51.4 us
    ppermute x20, waiting for transfers between devices, across(): lax.ppermute(lists[d], 'row', row_perm(0, d) if along_z else row_perm(d, 0))  48.2 us
    pallas_call x2, Pallas kernels, blend(): pl.pallas_call(functools.partial(blend_kernel, start, main, len(ys), with...  6.98 us
    ppermute x3, starting transfers between devices, shards(): lax.ppermute(so_far, 'col', [(c, c ^ step) for c in range(cols_n)])  6.15 us
    pallas_call x1, Pallas kernels, select_a(): pl.pallas_call(functools.partial(select_a_kernel, start, main), in_specs=...  3.15 us
  transfers between devices with their start and end apart: 23, of which 12 were waited for; matrix products, arithmetic and copies ran while one was open for 4% of the time, Pallas kernels for 8%

commit v1 on v0

--- a/solution.py
+++ b/solution.py
@@ -103,7 +103,7 @@
 def tiles(start, width, body):
     count = width // TILE
 
-    @pl.loop(0, count, unroll=next((n for n in (5, 4, 3) if count % n == 0), 1))
+    @pl.loop(0, count, unroll=next((n for n in (5, 4, 3, 7) if count % n == 0), 1))
     def _(t):
         body(pl.ds(pl.multiple_of(start + t * TILE, TILE), TILE))
 
@@ -332,10 +332,11 @@
     )(*args)
 
 
-def columns_kernel(mixed, keep, take, spread, p0, p1, p2, p3, out, stack, done, sem):
+def columns_kernel(mixed, keep, take, spread, *refs):
+    pieces, (out, stack, done, sem) = refs[:-4], refs[-4:]
     rows = mixed.shape[0]
     at = 0
-    for p in (p0, p1, p2, p3):
+    for p in pieces:
         for i in range(p.shape[0] // rows):
             stack[:, at * 128 : (at + 1) * 128] = p[i * rows : (i + 1) * rows, :]
             at += 1
@@ -353,7 +354,7 @@
 def columns(mixed, keep, take, spread, pieces):
     return pl.pallas_call(
         columns_kernel,
-        in_specs=[VMEM] * 8,
+        in_specs=[VMEM] * (4 + len(pieces)),
         out_specs=ANY,
         out_shape=jax.ShapeDtypeStruct(mixed.shape, BF),
         scratch_shapes=[
@@ -428,12 +429,11 @@
     )
     (rest_out,) = blend(place_b, keep, take, got_b, sim_rest, 0, SPLIT, (), into)
 
-    pieces = [mine]
-    step = 1
-    while step < cols_n:
-        so_far = jnp.concatenate(pieces, axis=0)
-        pieces.append(lax.ppermute(so_far, "col", [(c, c ^ step) for c in range(cols_n)]))
-        step *= 2
+    def crossed(piece, k):
+        return lax.ppermute(piece, "col", [(c, c ^ k) for c in range(cols_n)])
+
+    both = jnp.concatenate([mine, crossed(mine, 1)], axis=0)
+    pieces = [both] + [crossed(both, k) for k in range(2, cols_n, 2)]
     spread = join(
         hot((my_col ^ gone_col) * lane + col_rank, cols_n * lane), hot(last - my_col * wcols, wcols)
     )

time: 134 us -> 132 us (0.985)
  starting transfers between devices: 57.5 us -> 54.5 us
  local copies, waits for them, and re-layouts: 1.02 us -> 2.62 us
  waiting for transfers between devices: 49.6 us -> 51 us
    ppermute x20, starting transfers between devices: 51.4 us -> 45.8 us  [across(): lax.ppermute(lists[d], 'row', row_perm(0, d) if along_z else row_perm(d, 0))]
    ppermute x20, waiting for transfers between devices: 48.2 us -> 51 us  [across(): lax.ppermute(lists[d], 'row', row_perm(0, d) if along_z else row_perm(d, 0))]
    ppermute x3 -> x4, starting transfers between devices: 6.15 us -> 8.73 us  [crossed(): return lax.ppermute(piece, 'col', [(c, c ^ k) for c in range(cols_n)])]
    unnamed x8 -> x13, local copies, waits for them, and re-layouts: 1.01 us -> 2.6 us
    ppermute x3 -> x4, waiting for transfers between devices: 1.47 us -> 0.01 us  [crossed(): return lax.ppermute(piece, 'col', [(c, c ^ k) for c in range(cols_n)])]
  transfers between devices with their start and end apart: 23 -> 24, of which waited for: 12 -> 10; matrix products, arithmetic and copies ran while one was open for 4% -> 4% of each run, Pallas kernels for 8% -> 10%
where the time goes in v1:
time: 132 us
  starting transfers between devices  54.5 us (41%)
  waiting for transfers between devices  51 us (39%)
  Pallas kernels  15.2 us (12%)
  other arithmetic  4.68 us (4%)
  matrix products  2.8 us (2%)
  local copies, waits for them, and re-layouts  2.62 us (2%)
    ppermute x20, waiting for transfers between devices, across(): lax.ppermute(lists[d], 'row', row_perm(0, d) if along_z else row_perm(d, 0))  51 us
    ppermute x20, starting transfers between devices, across(): lax.ppermute(lists[d], 'row', row_perm(0, d) if along_z else row_perm(d, 0))  45.8 us
    ppermute x4, starting transfers between devices, crossed(): return lax.ppermute(piece, 'col', [(c, c ^ k) for c in range(cols_n)])  8.73 us
    pallas_call x2, Pallas kernels, blend(): pl.pallas_call(functools.partial(blend_kernel, start, main, len(ys), with...  6.97 us
    pallas_call x1, Pallas kernels, select_a(): pl.pallas_call(functools.partial(select_a_kernel, start, main), in_specs=...  3.02 us
  transfers between devices with their start and end apart: 24, of which 10 were waited for; matrix products, arithmetic and copies ran while one was open for 4% of the time, Pallas kernels for 10%

profile of v1, /device:TPU:1, one launch (start us, length us, event | category | flops | bytes accessed | tf_op | source)
XLA Modules:
  0.0 131.9 jit_solution(10312913428589159973)
XLA Ops:
  0.6 0.9 and_select_fusion.12
  1.5 0.7 compare_select_fusion.18
  2.3 0.4 convert_reduce_fusion.3
  3.0 2.6 %copy-done = bf16[192,14232]{1,0:T(8,128)(2,1)S(1)} copy-done((bf16[192,14232]{1,0:T(8,128)(2,1)S(1)}, bf16[192,14232]{1,0:T(8,128)(2,1)}, u32[]{:S(2)}) %copy-start) | copy-done | bytes 5465112
  5.6 0.9 select_b.1.refs_1_
  6.5 3.6 %collective-permute-start.16 = (bf16[48,3840]{1,0:T(8,128)(2,1)S(1)}, bf16[48,3840]{1,0:T(8,128)(2,1)S(1)}, u32[]{:S(2)}, u32[]{:S(2)}) collective-permute-start(bf16[48,3840]{1,0:T(8,128)(2,1)S(1)} %select_b.1.refs_1_), channel_id=1, source_target_pairs={{0,192},{8,200},{16,208},{24,216},{32,224},{40,232},{48,240},{56,2... | collective-permute-start | bytes 1105928 | tf_op jit(solution)/shard_map/ppermute | solution.py:415
  10.1 0.4 convert_reduce_fusion.2
  10.6 0.3 shard_map.60.refs_0_
  10.9 3.0 %select_a.1 = (bf16[24,3840]{1,0:T(8,128)(2,1)S(1)}, bf16[24,3840]{1,0:T(8,128)(2,1)S(1)}, bf16[24,3840]{1,0:T(8,128)(2,1)S(1)}, bf16[24,3840]{1,0:T(8,128)(2,1)...) custom-call(bf16[192,192]{1,0:T(8,128)(2,1)S(1)} %shard_map.60.refs_, ...), custom_call_target="tpu_custom_call" | custom-call | flops 566231040 | bytes 2949120 | tf_op jit(solution)/shard_map/select_a/pallas_call | solution.py:158
  13.9 1.7 %collective-permute-start = (bf16[24,3840]{1,0:T(8,128)(2,1)S(1)}, bf16[24,3840]{1,0:T(8,128)(2,1)S(1)}, u32[]{:S(2)}, u32[]{:S(2)}) collective-permute-start(bf16[24,3840]{1,0:T(8,128)(2,1)S(1)} %get-tuple-element.36), channel_id=1, source_target_pairs={{0,8},{8,16},{16,24},{24,32},{32,40},{40,48},{48,56},{56,0},{64,72... | collective-permute-start | bytes 552968 | tf_op jit(solution)/shard_map/ppermute | solution.py:415
  15.6 3.0 %collective-permute-start.1 = (bf16[24,3840]{1,0:T(8,128)(2,1)S(1)}, bf16[24,3840]{1,0:T(8,128)(2,1)S(1)}, u32[]{:S(2)}, u32[]{:S(2)}) collective-permute-start(bf16[24,3840]{1,0:T(8,128)(2,1)S(1)} %get-tuple-element.37), channel_id=1, source_target_pairs={{0,16},{8,24},{16,32},{24,40},{32,48},{40,56},{48,0},{56,8},{64,80... | collective-permute-start | bytes 552968 | tf_op jit(solution)/shard_map/ppermute | solution.py:415
  18.6 3.8 %collective-permute-start.2 = (bf16[24,3840]{1,0:T(8,128)(2,1)S(1)}, bf16[24,3840]{1,0:T(8,128)(2,1)S(1)}, u32[]{:S(2)}, u32[]{:S(2)}) collective-permute-start(bf16[24,3840]{1,0:T(8,128)(2,1)S(1)} %get-tuple-element.38), channel_id=1, source_target_pairs={{0,24},{8,32},{16,40},{24,48},{32,56},{40,0},{48,8},{56,16},{64,88... | collective-permute-start | bytes 552968 | tf_op jit(solution)/shard_map/ppermute | solution.py:415
  22.4 0.5 collective-permute-start.3
  22.9 0.4 convert_reduce_fusion.1
  23.2 0.4 convert_reduce_fusion.4
  23.6 0.4 convert_reduce_fusion.5
  24.6 1.0 fusion.2
  25.6 0.6 fusion.13.refs_9_
  26.2 0.5 shard_map.59
  26.7 4.5 %collective-permute-start.4 = (bf16[24,3840]{1,0:T(8,128)(2,1)S(1)}, bf16[24,3840]{1,0:T(8,128)(2,1)S(1)}, u32[]{:S(2)}, u32[]{:S(2)}) collective-permute-start(bf16[24,3840]{1,0:T(8,128)(2,1)S(1)} %get-tuple-element.40), channel_id=1, source_target_pairs={{0,40},{8,48},{16,56},{24,0},{32,8},{40,16},{48,24},{56,32},{64,10... | collective-permute-start | bytes 552968 | tf_op jit(solution)/shard_map/ppermute | solution.py:415
  31.3 2.4 %collective-permute-start.5 = (bf16[24,3840]{1,0:T(8,128)(2,1)S(1)}, bf16[24,3840]{1,0:T(8,128)(2,1)S(1)}, u32[]{:S(2)}, u32[]{:S(2)}) collective-permute-start(bf16[24,3840]{1,0:T(8,128)(2,1)S(1)} %get-tuple-element.41), channel_id=1, source_target_pairs={{0,48},{8,56},{16,0},{24,8},{32,16},{40,24},{48,32},{56,40},{64,11... | collective-permute-start | bytes 552968 | tf_op jit(solution)/shard_map/ppermute | solution.py:415
  33.7 9.1 %collective-permute-done.2.refs_4_ = bf16[24,3840]{1,0:T(8,128)(2,1)S(1)} collective-permute-done((bf16[24,3840]{1,0:T(8,128)(2,1)S(1)}, bf16[24,3840]{1,0:T(8,128)(2,1)S(1)}, u32[]{:S(2)}, u32[]{:S(2)}) %collective-permute-start.2) | collective-permute-done | bytes 184352 | tf_op jit(solution)/shard_map/ppermute | solution.py:415
  42.8 4.2 %collective-permute-done.3.refs_5_ = bf16[24,3840]{1,0:T(8,128)(2,1)S(1)} collective-permute-done((bf16[24,3840]{1,0:T(8,128)(2,1)S(1)}, bf16[24,3840]{1,0:T(8,128)(2,1)S(1)}, u32[]{:S(2)}, u32[]{:S(2)}) %collective-permute-start.3) | collective-permute-done | bytes 184352 | tf_op jit(solution)/shard_map/ppermute | solution.py:415
  47.0 0.3 collective-permute-start.15
  47.4 0.7 collective-permute-start.14
  48.1 7.3 %collective-permute-done.5.refs_7_ = bf16[24,3840]{1,0:T(8,128)(2,1)S(1)} collective-permute-done((bf16[24,3840]{1,0:T(8,128)(2,1)S(1)}, bf16[24,3840]{1,0:T(8,128)(2,1)S(1)}, u32[]{:S(2)}, u32[]{:S(2)}) %collective-permute-start.5) | collective-permute-done | bytes 184352 | tf_op jit(solution)/shard_map/ppermute | solution.py:415
  55.3 2.0 %collective-permute-done.6.refs_8_ = bf16[24,3840]{1,0:T(8,128)(2,1)S(1)} collective-permute-done((bf16[24,3840]{1,0:T(8,128)(2,1)S(1)}, bf16[24,3840]{1,0:T(8,128)(2,1)S(1)}, u32[]{:S(2)}, u32[]{:S(2)}) %collective-permute-start.6) | collective-permute-done | bytes 184352 | tf_op jit(solution)/shard_map/ppermute | solution.py:415
  57.3 0.9 turn.2
  58.3 1.6 %collective-permute-start.8 = (bf16[48,3840]{1,0:T(8,128)(2,1)S(1)}, bf16[48,3840]{1,0:T(8,128)(2,1)S(1)}, u32[]{:S(2)}, u32[]{:S(2)}) collective-permute-start(bf16[48,3840]{1,0:T(8,128)(2,1)S(1)} %get-tuple-element.45), channel_id=1, source_target_pairs={{0,128},{8,136},{16,144},{24,152},{32,160},{40,168},{48,176},{56,1... | collective-permute-start | bytes 1105928 | tf_op jit(solution)/shard_map/ppermute | solution.py:415
  59.9 1.0 collective-permute-start.9
  61.2 1.7 %fusion.9.spread = bf16[1024,768]{1,0:T(8,128)(2,1)S(1)} fusion(s32[768]{0:T(1024)S(1)} %multiply_add_fusion, s32[768]{0:T(1024)S(1)} %get-tuple-element.105), kind=kOutput, calls=%fused_computation.22 | convolution fusion | flops 1210122240 | bytes 1579008 | tf_op jit(solution)/shard_map/dot_general | solution.py:43
  62.9 4.0 %collective-permute-done.14.refs_2_ = bf16[48,3840]{1,0:T(8,128)(2,1)S(1)} collective-permute-done((bf16[48,3840]{1,0:T(8,128)(2,1)S(1)}, bf16[48,3840]{1,0:T(8,128)(2,1)S(1)}, u32[]{:S(2)}, u32[]{:S(2)}) %collective-permute-start.14) | collective-permute-done | bytes 368672 | tf_op jit(solution)/shard_map/ppermute | solution.py:415
  67.0 0.9 turn.3
  67.9 7.3 %collective-permute-start.18 = (bf16[24,3840]{1,0:T(8,128)(2,1)S(1)}, bf16[24,3840]{1,0:T(8,128)(2,1)S(1)}, u32[]{:S(2)}, u32[]{:S(2)}) collective-permute-start(bf16[24,3840]{1,0:T(8,128)(2,1)S(1)} %get-tuple-element.53), channel_id=1, source_target_pairs={{0,16},{8,24},{16,32},{24,40},{32,48},{40,56},{48,0},{56,8},{64,80... | collective-permute-start | bytes 552968 | tf_op jit(solution)/shard_map/ppermute | solution.py:415
  75.3 2.0 %collective-permute-done.7.refs_5_ = bf16[48,3840]{1,0:T(8,128)(2,1)S(1)} collective-permute-done((bf16[48,3840]{1,0:T(8,128)(2,1)S(1)}, bf16[48,3840]{1,0:T(8,128)(2,1)S(1)}, u32[]{:S(2)}, u32[]{:S(2)}) %collective-permute-start.7) | collective-permute-done | bytes 368672 | tf_op jit(solution)/shard_map/ppermute | solution.py:415
  77.3 3.0 %collective-permute-done.8.refs_6_ = bf16[48,3840]{1,0:T(8,128)(2,1)S(1)} collective-permute-done((bf16[48,3840]{1,0:T(8,128)(2,1)S(1)}, bf16[48,3840]{1,0:T(8,128)(2,1)S(1)}, u32[]{:S(2)}, u32[]{:S(2)}) %collective-permute-start.8) | collective-permute-done | bytes 368672 | tf_op jit(solution)/shard_map/ppermute | solution.py:415
  80.3 3.3 %blend.2 = (bf16[192,14232]{1,0:T(8,128)(2,1)}, bf16[192,768]{1,0:T(8,128)(2,1)S(1)}, bf16[192,128]{1,0:T(8,128)(2,1)S(1)}) custom-call(bf16[192,192]{1,0:T(8,128)(2,1)S(1)} %get-tuple-element.31.refs_0_, f32[192,1]{1,0:T(8,128)S(1)} %get-tuple-element.32.refs_1_, f32[192,1]{1,0:T(8,128)S(1)} %get-tuple-element.33.refs_2_, bf16[192,14232]{1,0:T(8,128)(2,1)S(1)} %bitcast.17, ...), custom_call_target="tpu_custom_call" | custom-call | flops 1132462080 | bytes 2949120 | tf_op jit(solution)/shard_map/blend/pallas_call | solution.py:313
  83.6 3.1 %collective-permute-start.10 = (bf16[192,128]{1,0:T(8,128)(2,1)S(1)}, bf16[192,128]{1,0:T(8,128)(2,1)S(1)}, u32[]{:S(2)}, u32[]{:S(2)}) collective-permute-start(bf16[192,128]{1,0:T(8,128)(2,1)S(1)} %get-tuple-element.48), channel_id=1, source_target_pairs={{0,1},{1,0},{2,3},{3,2},{4,5},{5,4},{6,7},{7,6},{8,9},{9,8},{10,11... | collective-permute-start | bytes 147464 | tf_op jit(solution)/shard_map/ppermute | solution.py:433
  86.8 11.2 %collective-permute-start.20 = (bf16[24,3840]{1,0:T(8,128)(2,1)S(1)}, bf16[24,3840]{1,0:T(8,128)(2,1)S(1)}, u32[]{:S(2)}, u32[]{:S(2)}) collective-permute-start(bf16[24,3840]{1,0:T(8,128)(2,1)S(1)} %get-tuple-element.55), channel_id=1, source_target_pairs={{0,32},{8,40},{16,48},{24,56},{32,0},{40,8},{48,16},{56,24},{64,96... | collective-permute-start | bytes 552968 | tf_op jit(solution)/shard_map/ppermute | solution.py:415
  98.1 3.8 %collective-permute-start.22 = (bf16[24,3840]{1,0:T(8,128)(2,1)S(1)}, bf16[24,3840]{1,0:T(8,128)(2,1)S(1)}, u32[]{:S(2)}, u32[]{:S(2)}) collective-permute-start(bf16[24,3840]{1,0:T(8,128)(2,1)S(1)} %get-tuple-element.57), channel_id=1, source_target_pairs={{0,48},{8,56},{16,0},{24,8},{32,16},{40,24},{48,32},{56,40},{64,11... | collective-permute-start | bytes 552968 | tf_op jit(solution)/shard_map/ppermute | solution.py:415
  101.9 2.6 %collective-permute-start.13 = (bf16[384,128]{1,0:T(8,128)(2,1)S(1)}, bf16[384,128]{1,0:T(8,128)(2,1)S(1)}, u32[]{:S(2)}, u32[]{:S(2)}) collective-permute-start(bf16[384,128]{1,0:T(8,128)(2,1)S(1)} %constant_dynamic-update-slice_fusion.refs_0_), channel_id=1, source_target_pairs={{0,6},{1,7},{2,4},{3,5},{4,2},{5,3},{6,0},{7,1},{8,14},{9,15},{10,... | collective-permute-start | bytes 294920 | tf_op jit(solution)/shard_map/ppermute | solution.py:433
  104.5 14.0 %collective-permute-done.20.refs_8_ = bf16[24,3840]{1,0:T(8,128)(2,1)S(1)} collective-permute-done((bf16[24,3840]{1,0:T(8,128)(2,1)S(1)}, bf16[24,3840]{1,0:T(8,128)(2,1)S(1)}, u32[]{:S(2)}, u32[]{:S(2)}) %collective-permute-start.20) | collective-permute-done | bytes 184352 | tf_op jit(solution)/shard_map/ppermute | solution.py:415
  118.5 2.8 %collective-permute-start.12 = (bf16[384,128]{1,0:T(8,128)(2,1)S(1)}, bf16[384,128]{1,0:T(8,128)(2,1)S(1)}, u32[]{:S(2)}, u32[]{:S(2)}) collective-permute-start(bf16[384,128]{1,0:T(8,128)(2,1)S(1)} %constant_dynamic-update-slice_fusion.refs_0_), channel_id=1, source_target_pairs={{0,4},{1,5},{2,6},{3,7},{4,0},{5,1},{6,2},{7,3},{8,12},{9,13},{10,... | collective-permute-start | bytes 294920 | tf_op jit(solution)/shard_map/ppermute | solution.py:433
  121.2 0.3 collective-permute-start.11
  121.5 0.3 collective-permute-done.22.refs_10_
  121.9 5.0 %collective-permute-done.23.refs_11_ = bf16[24,3840]{1,0:T(8,128)(2,1)S(1)} collective-permute-done((bf16[24,3840]{1,0:T(8,128)(2,1)S(1)}, bf16[24,3840]{1,0:T(8,128)(2,1)S(1)}, u32[]{:S(2)}, u32[]{:S(2)}) %collective-permute-start.23) | collective-permute-done | bytes 184352 | tf_op jit(solution)/shard_map/ppermute | solution.py:415
  126.8 3.7 %blend.3 = bf16[192,14232]{1,0:T(8,128)(2,1)} custom-call(bf16[192,192]{1,0:T(8,128)(2,1)S(1)} %get-tuple-element.49.refs_0_, f32[192,1]{1,0:T(8,128)S(1)} %get-tuple-element.32.refs_1_, f32[192,1]{1,0:T(8,128)S(1)} %get-tuple-element.33.refs_2_, bf16[192,14232]{1,0:T(8,128)(2,1)S(1)} %bitcast.17, ...), custom_call_target="tpu_custom_call", output_to_operand_aliasing={{}: (12, {})} | custom-call | flops 1132462080 | bytes 2949120 | tf_op jit(solution)/shard_map/blend/pallas_call | solution.py:313
  130.5 1.3 columns.1
  (52 shorter events, 1.6 us)
Async XLA Ops:
  2.9 2.6 %copy-start = (bf16[192,14232]{1,0:T(8,128)(2,1)S(1)}, bf16[192,14232]{1,0:T(8,128)(2,1)}, u32[]{:S(2)}) copy-start(bf16[192,14232]{1,0:T(8,128)(2,1)} %refs_3_.3) | copy-start | bytes 16395268
  5.6 4.9 %copy-start.2 = (s32[768,2]{0,1:T(2,128)S(1)}, s32[768,2]{0,1:T(2,128)}, u32[]{:S(2)}) copy-start(s32[768,2]{0,1:T(2,128)} %param.6) | copy-start | bytes 18436
  5.6 5.3 %copy-start.1 = (bf16[192,768]{1,0:T(8,128)(2,1)S(1)}, bf16[192,768]{1,0:T(8,128)(2,1)}, u32[]{:S(2)}) copy-start(bf16[192,768]{1,0:T(8,128)(2,1)} %refs_8_.1) | copy-start | bytes 884740
  6.5 53.5 %collective-permute-start.16 = (bf16[48,3840]{1,0:T(8,128)(2,1)S(1)}, bf16[48,3840]{1,0:T(8,128)(2,1)S(1)}, u32[]{:S(2)}, u32[]{:S(2)}) collective-permute-start(bf16[48,3840]{1,0:T(8,128)(2,1)S(1)} %select_b.1.refs_1_), channel_id=1, source_target_pairs={{0,192},{8,200},{16,208},{24,216},{32,224},{40,232},{48,240},{56,2... | collective-permute-start | bytes 1105928 | tf_op jit(solution)/shard_map/ppermute | solution.py:415
  10.9 13.1 %copy-start.3 = (s32[6144]{0:T(1024)S(1)}, s32[6144]{0:T(1024)}, u32[]{:S(2)}) copy-start(s32[6144]{0:T(1024)} %param.7) | copy-start | bytes 73732
  13.9 12.8 %collective-permute-start = (bf16[24,3840]{1,0:T(8,128)(2,1)S(1)}, bf16[24,3840]{1,0:T(8,128)(2,1)S(1)}, u32[]{:S(2)}, u32[]{:S(2)}) collective-permute-start(bf16[24,3840]{1,0:T(8,128)(2,1)S(1)} %get-tuple-element.36), channel_id=1, source_target_pairs={{0,8},{8,16},{16,24},{24,32},{32,40},{40,48},{48,56},{56,0},{64,72... | collective-permute-start | bytes 552968 | tf_op jit(solution)/shard_map/ppermute | solution.py:415
  15.6 15.6 %collective-permute-start.1 = (bf16[24,3840]{1,0:T(8,128)(2,1)S(1)}, bf16[24,3840]{1,0:T(8,128)(2,1)S(1)}, u32[]{:S(2)}, u32[]{:S(2)}) collective-permute-start(bf16[24,3840]{1,0:T(8,128)(2,1)S(1)} %get-tuple-element.37), channel_id=1, source_target_pairs={{0,16},{8,24},{16,32},{24,40},{32,48},{40,56},{48,0},{56,8},{64,80... | collective-permute-start | bytes 552968 | tf_op jit(solution)/shard_map/ppermute | solution.py:415
  18.6 24.2 %collective-permute-start.2 = (bf16[24,3840]{1,0:T(8,128)(2,1)S(1)}, bf16[24,3840]{1,0:T(8,128)(2,1)S(1)}, u32[]{:S(2)}, u32[]{:S(2)}) collective-permute-start(bf16[24,3840]{1,0:T(8,128)(2,1)S(1)} %get-tuple-element.38), channel_id=1, source_target_pairs={{0,24},{8,32},{16,40},{24,48},{32,56},{40,0},{48,8},{56,16},{64,88... | collective-permute-start | bytes 552968 | tf_op jit(solution)/shard_map/ppermute | solution.py:415
  22.4 24.7 %collective-permute-start.3 = (bf16[24,3840]{1,0:T(8,128)(2,1)S(1)}, bf16[24,3840]{1,0:T(8,128)(2,1)S(1)}, u32[]{:S(2)}, u32[]{:S(2)}) collective-permute-start(bf16[24,3840]{1,0:T(8,128)(2,1)S(1)} %get-tuple-element.39), channel_id=1, source_target_pairs={{0,32},{8,40},{16,48},{24,56},{32,0},{40,8},{48,16},{56,24},{64,96... | collective-permute-start | bytes 552968 | tf_op jit(solution)/shard_map/ppermute | solution.py:415
  26.7 20.7 %collective-permute-start.4 = (bf16[24,3840]{1,0:T(8,128)(2,1)S(1)}, bf16[24,3840]{1,0:T(8,128)(2,1)S(1)}, u32[]{:S(2)}, u32[]{:S(2)}) collective-permute-start(bf16[24,3840]{1,0:T(8,128)(2,1)S(1)} %get-tuple-element.40), channel_id=1, source_target_pairs={{0,40},{8,48},{16,56},{24,0},{32,8},{40,16},{48,24},{56,32},{64,10... | collective-permute-start | bytes 552968 | tf_op jit(solution)/shard_map/ppermute | solution.py:415
  31.3 24.1 %collective-permute-start.5 = (bf16[24,3840]{1,0:T(8,128)(2,1)S(1)}, bf16[24,3840]{1,0:T(8,128)(2,1)S(1)}, u32[]{:S(2)}, u32[]{:S(2)}) collective-permute-start(bf16[24,3840]{1,0:T(8,128)(2,1)S(1)} %get-tuple-element.41), channel_id=1, source_target_pairs={{0,48},{8,56},{16,0},{24,8},{32,16},{40,24},{48,32},{56,40},{64,11... | collective-permute-start | bytes 552968 | tf_op jit(solution)/shard_map/ppermute | solution.py:415
  42.8 14.5 %collective-permute-start.6 = (bf16[24,3840]{1,0:T(8,128)(2,1)S(1)}, bf16[24,3840]{1,0:T(8,128)(2,1)S(1)}, u32[]{:S(2)}, u32[]{:S(2)}) collective-permute-start(bf16[24,3840]{1,0:T(8,128)(2,1)S(1)} %get-tuple-element.42), channel_id=1, source_target_pairs={{0,56},{8,0},{16,8},{24,16},{32,24},{40,32},{48,40},{56,48},{64,12... | collective-permute-start | bytes 552968 | tf_op jit(solution)/shard_map/ppermute | solution.py:415
  47.0 15.9 %collective-permute-start.15 = (bf16[48,3840]{1,0:T(8,128)(2,1)S(1)}, bf16[48,3840]{1,0:T(8,128)(2,1)S(1)}, u32[]{:S(2)}, u32[]{:S(2)}) collective-permute-start(bf16[48,3840]{1,0:T(8,128)(2,1)S(1)} %select_b.1.refs_1_), channel_id=1, source_target_pairs={{0,128},{8,136},{16,144},{24,152},{32,160},{40,168},{48,176},{56,1... | collective-permute-start | bytes 1105928 | tf_op jit(solution)/shard_map/ppermute | solution.py:415
  47.4 19.6 %collective-permute-start.14 = (bf16[48,3840]{1,0:T(8,128)(2,1)S(1)}, bf16[48,3840]{1,0:T(8,128)(2,1)S(1)}, u32[]{:S(2)}, u32[]{:S(2)}) collective-permute-start(bf16[48,3840]{1,0:T(8,128)(2,1)S(1)} %select_b.1.refs_1_), channel_id=1, source_target_pairs={{0,64},{8,72},{16,80},{24,88},{32,96},{40,104},{48,112},{56,120},{... | collective-permute-start | bytes 1105928 | tf_op jit(solution)/shard_map/ppermute | solution.py:415
  57.3 23.0 %slice-start = ((s8[5505024]{0:T(1024)(128)(4,1)}), s8[4194304]{0:T(1024)(128)(4,1)S(1)}, s32[]{:S(2)}) async-start(s8[5505024]{0:T(1024)(128)(4,1)} %bitcast.16), calls=%async_computation | async-start | bytes 8388608
  58.2 19.1 %collective-permute-start.7 = (bf16[48,3840]{1,0:T(8,128)(2,1)S(1)}, bf16[48,3840]{1,0:T(8,128)(2,1)S(1)}, u32[]{:S(2)}, u32[]{:S(2)}) collective-permute-start(bf16[48,3840]{1,0:T(8,128)(2,1)S(1)} %get-tuple-element.44), channel_id=1, source_target_pairs={{0,64},{8,72},{16,80},{24,88},{32,96},{40,104},{48,112},{56,120},{... | collective-permute-start | bytes 1105928 | tf_op jit(solution)/shard_map/ppermute | solution.py:415
  58.3 22.0 %collective-permute-start.8 = (bf16[48,3840]{1,0:T(8,128)(2,1)S(1)}, bf16[48,3840]{1,0:T(8,128)(2,1)S(1)}, u32[]{:S(2)}, u32[]{:S(2)}) collective-permute-start(bf16[48,3840]{1,0:T(8,128)(2,1)S(1)} %get-tuple-element.45), channel_id=1, source_target_pairs={{0,128},{8,136},{16,144},{24,152},{32,160},{40,168},{48,176},{56,1... | collective-permute-start | bytes 1105928 | tf_op jit(solution)/shard_map/ppermute | solution.py:415
  59.9 20.4 %collective-permute-start.9 = (bf16[48,3840]{1,0:T(8,128)(2,1)S(1)}, bf16[48,3840]{1,0:T(8,128)(2,1)S(1)}, u32[]{:S(2)}, u32[]{:S(2)}) collective-permute-start(bf16[48,3840]{1,0:T(8,128)(2,1)S(1)} %get-tuple-element.46), channel_id=1, source_target_pairs={{0,192},{8,200},{16,208},{24,216},{32,224},{40,232},{48,240},{56,2... | collective-permute-start | bytes 1105928 | tf_op jit(solution)/shard_map/ppermute | solution.py:415
  61.2 19.1 %slice-start.1 = ((s8[5505024]{0:T(1024)(128)(4,1)}), s8[1310720]{0:T(1024)(128)(4,1)S(1)}, s32[]{:S(2)}) async-start(s8[5505024]{0:T(1024)(128)(4,1)} %bitcast.16), calls=%async_computation.1 | async-start | bytes 2621440
  67.8 30.2 %collective-permute-start.17 = (bf16[24,3840]{1,0:T(8,128)(2,1)S(1)}, bf16[24,3840]{1,0:T(8,128)(2,1)S(1)}, u32[]{:S(2)}, u32[]{:S(2)}) collective-permute-start(bf16[24,3840]{1,0:T(8,128)(2,1)S(1)} %get-tuple-element.52), channel_id=1, source_target_pairs={{0,8},{8,16},{16,24},{24,32},{32,40},{40,48},{48,56},{56,0},{64,72... | collective-permute-start | bytes 552968 | tf_op jit(solution)/shard_map/ppermute | solution.py:415
  67.9 30.1 %collective-permute-start.18 = (bf16[24,3840]{1,0:T(8,128)(2,1)S(1)}, bf16[24,3840]{1,0:T(8,128)(2,1)S(1)}, u32[]{:S(2)}, u32[]{:S(2)}) collective-permute-start(bf16[24,3840]{1,0:T(8,128)(2,1)S(1)} %get-tuple-element.53), channel_id=1, source_target_pairs={{0,16},{8,24},{16,32},{24,40},{32,48},{40,56},{48,0},{56,8},{64,80... | collective-permute-start | bytes 552968 | tf_op jit(solution)/shard_map/ppermute | solution.py:415
  83.6 18.2 %collective-permute-start.10 = (bf16[192,128]{1,0:T(8,128)(2,1)S(1)}, bf16[192,128]{1,0:T(8,128)(2,1)S(1)}, u32[]{:S(2)}, u32[]{:S(2)}) collective-permute-start(bf16[192,128]{1,0:T(8,128)(2,1)S(1)} %get-tuple-element.48), channel_id=1, source_target_pairs={{0,1},{1,0},{2,3},{3,2},{4,5},{5,4},{6,7},{7,6},{8,9},{9,8},{10,11... | collective-permute-start | bytes 147464 | tf_op jit(solution)/shard_map/ppermute | solution.py:433
  86.7 15.1 %collective-permute-start.19 = (bf16[24,3840]{1,0:T(8,128)(2,1)S(1)}, bf16[24,3840]{1,0:T(8,128)(2,1)S(1)}, u32[]{:S(2)}, u32[]{:S(2)}) collective-permute-start(bf16[24,3840]{1,0:T(8,128)(2,1)S(1)} %get-tuple-element.54), channel_id=1, source_target_pairs={{0,24},{8,32},{16,40},{24,48},{32,56},{40,0},{48,8},{56,16},{64,88... | collective-permute-start | bytes 552968 | tf_op jit(solution)/shard_map/ppermute | solution.py:415
  86.8 31.6 %collective-permute-start.20 = (bf16[24,3840]{1,0:T(8,128)(2,1)S(1)}, bf16[24,3840]{1,0:T(8,128)(2,1)S(1)}, u32[]{:S(2)}, u32[]{:S(2)}) collective-permute-start(bf16[24,3840]{1,0:T(8,128)(2,1)S(1)} %get-tuple-element.55), channel_id=1, source_target_pairs={{0,32},{8,40},{16,48},{24,56},{32,0},{40,8},{48,16},{56,24},{64,96... | collective-permute-start | bytes 552968 | tf_op jit(solution)/shard_map/ppermute | solution.py:415
  98.1 23.2 %collective-permute-start.21 = (bf16[24,3840]{1,0:T(8,128)(2,1)S(1)}, bf16[24,3840]{1,0:T(8,128)(2,1)S(1)}, u32[]{:S(2)}, u32[]{:S(2)}) collective-permute-start(bf16[24,3840]{1,0:T(8,128)(2,1)S(1)} %get-tuple-element.56), channel_id=1, source_target_pairs={{0,40},{8,48},{16,56},{24,0},{32,8},{40,16},{48,24},{56,32},{64,10... | collective-permute-start | bytes 552968 | tf_op jit(solution)/shard_map/ppermute | solution.py:415
  98.1 23.8 %collective-permute-start.22 = (bf16[24,3840]{1,0:T(8,128)(2,1)S(1)}, bf16[24,3840]{1,0:T(8,128)(2,1)S(1)}, u32[]{:S(2)}, u32[]{:S(2)}) collective-permute-start(bf16[24,3840]{1,0:T(8,128)(2,1)S(1)} %get-tuple-element.57), channel_id=1, source_target_pairs={{0,48},{8,56},{16,0},{24,8},{32,16},{40,24},{48,32},{56,40},{64,11... | collective-permute-start | bytes 552968 | tf_op jit(solution)/shard_map/ppermute | solution.py:415
  101.8 25.0 %collective-permute-start.23 = (bf16[24,3840]{1,0:T(8,128)(2,1)S(1)}, bf16[24,3840]{1,0:T(8,128)(2,1)S(1)}, u32[]{:S(2)}, u32[]{:S(2)}) collective-permute-start(bf16[24,3840]{1,0:T(8,128)(2,1)S(1)} %get-tuple-element.58), channel_id=1, source_target_pairs={{0,56},{8,0},{16,8},{24,16},{32,24},{40,32},{48,40},{56,48},{64,12... | collective-permute-start | bytes 552968 | tf_op jit(solution)/shard_map/ppermute | solution.py:415
  101.9 28.6 %collective-permute-start.13 = (bf16[384,128]{1,0:T(8,128)(2,1)S(1)}, bf16[384,128]{1,0:T(8,128)(2,1)S(1)}, u32[]{:S(2)}, u32[]{:S(2)}) collective-permute-start(bf16[384,128]{1,0:T(8,128)(2,1)S(1)} %constant_dynamic-update-slice_fusion.refs_0_), channel_id=1, source_target_pairs={{0,6},{1,7},{2,4},{3,5},{4,2},{5,3},{6,0},{7,1},{8,14},{9,15},{10,... | collective-permute-start | bytes 294920 | tf_op jit(solution)/shard_map/ppermute | solution.py:433
  118.5 12.1 %collective-permute-start.12 = (bf16[384,128]{1,0:T(8,128)(2,1)S(1)}, bf16[384,128]{1,0:T(8,128)(2,1)S(1)}, u32[]{:S(2)}, u32[]{:S(2)}) collective-permute-start(bf16[384,128]{1,0:T(8,128)(2,1)S(1)} %constant_dynamic-update-slice_fusion.refs_0_), channel_id=1, source_target_pairs={{0,4},{1,5},{2,6},{3,7},{4,0},{5,1},{6,2},{7,3},{8,12},{9,13},{10,... | collective-permute-start | bytes 294920 | tf_op jit(solution)/shard_map/ppermute | solution.py:433
  121.2 9.3 %collective-permute-start.11 = (bf16[384,128]{1,0:T(8,128)(2,1)S(1)}, bf16[384,128]{1,0:T(8,128)(2,1)S(1)}, u32[]{:S(2)}, u32[]{:S(2)}) collective-permute-start(bf16[384,128]{1,0:T(8,128)(2,1)S(1)} %constant_dynamic-update-slice_fusion.refs_0_), channel_id=1, source_target_pairs={{0,2},{1,3},{2,0},{3,1},{4,6},{5,7},{6,4},{7,5},{8,10},{9,11},{10,... | collective-permute-start | bytes 294920 | tf_op jit(solution)/shard_map/ppermute | solution.py:433
